TPU v7x, 32 devices: a whole 2x2x4 slice. The times are simulated.
32 devices in a mesh: dom: 4 (over x, core), grp: 8 (over z, y).
Axes of the slice: x: 2, y: 2, z: 4, core: 2. Of those that a mesh axis runs over, the one named last changes fastest.
Arguments:
- features: bfloat16 [131072, 256], P(('dom', 'grp')), may hold values from -6 to 6
- w_fine: bfloat16 [256, 256], replicated, may hold values from -0.375 to 0.375
- adj_tiles: bfloat16 [1024, 20, 128, 128], P(('dom', 'grp')), may hold values from -0.125 to 0.125
- tile_cols: int32 [1024, 20], P(('dom', 'grp')), may hold values from 0 to 39
- tile_count: int32 [1024], P(('dom', 'grp')), may hold values from 1 to 20, as said below
- send_lower: int32 [128], P(('dom', 'grp')), may hold values from 0 to 31
- send_upper: int32 [128], P(('dom', 'grp')), may hold values from 0 to 31
- assign: int32 [131072], P(('dom', 'grp')), may hold values from 0 to 1023, as said below
- w_coarse: bfloat16 [256, 256], replicated, may hold values from -0.375 to 0.375
- coarse_adj: bfloat16 [1024, 1024], P(('dom', 'grp')), may hold values from -0.1875 to 0.1875
Outputs:
- output: bfloat16 [131072, 256], P(('dom', 'grp'))
Inputs may be any that keep to these rules, and one draw needn't show every extreme that they name: The first tile_count[r] slots of block row r are live; the others are ignored. `assign`: every coarse node is the coarse node of at least one vertex.
All inputs are finite; a program needn't handle non-finite values.
Results may differ from a plain program's by a relative error of at most 0.011.
Values may be sent and summed in bfloat16 or wider, within the bound.
No kernel may reach another device: no remote copies, remote signals or barrier semaphores. Data moves between devices by JAX's collectives and lax.ppermute only.
A program may use at most 192 MiB of HBM per device.

v0:
```python
import jax
import jax.numpy as jnp
from jax import lax
from jax.sharding import PartitionSpec as P

NC = 1024


def with_halo(shard, sides, width):
    for axis, dim in sides:
        peers, length = (lax.axis_size(axis), shard.shape[dim])
        up = [(i, (i + 1) % peers) for i in range(peers)]
        down = [(j, i) for i, j in up]
        last = lax.slice_in_dim(shard, length - width, length, axis=dim)
        initial = lax.slice_in_dim(shard, 0, width, axis=dim)
        before = lax.ppermute(last, axis, up)
        after = lax.ppermute(initial, axis, down)
        shard = jnp.concatenate([before, shard, after], axis=dim)
    return shard


def finish(coarse_sums, counts, w_coarse):
    coarse = (coarse_sums / jnp.sqrt(counts)[:, None]).astype(jnp.bfloat16)
    return jnp.dot(coarse, w_coarse, preferred_element_type=jnp.float32).astype(jnp.bfloat16)


def per_device(
    features,
    w_fine,
    adj_tiles,
    tile_cols,
    tile_count,
    send_lower,
    send_upper,
    assign,
    w_coarse,
    coarse_adj,
):
    vertex_rows = features.shape[0]
    feat_width = features.shape[1]
    block_rows = adj_tiles.shape[2]
    slot_count = adj_tiles.shape[1]
    block_count = vertex_rows // block_rows
    halo_blocks = send_lower.shape[0]
    projected = jnp.dot(features, w_fine, preferred_element_type=jnp.float32).astype(jnp.bfloat16)
    own_blocks = projected.reshape(block_count, block_rows, feat_width)
    lower_sel = own_blocks[send_lower]
    upper_sel = own_blocks[send_upper]
    packed = jnp.concatenate([lower_sel, upper_sel], axis=0).reshape(
        2 * halo_blocks * block_rows, feat_width
    )
    padded = with_halo(packed, (("dom", 0),), halo_blocks * block_rows)
    from_below = padded[: halo_blocks * block_rows].reshape(halo_blocks, block_rows, feat_width)
    from_above = padded[-halo_blocks * block_rows :].reshape(halo_blocks, block_rows, feat_width)
    extended = jnp.concatenate([own_blocks, from_below, from_above], axis=0)
    coarse_sums = jax.ops.segment_sum(features.astype(jnp.float32), assign, num_segments=NC)
    counts = jax.ops.segment_sum(jnp.ones((vertex_rows,), jnp.float32), assign, num_segments=NC)
    live_mask = jnp.arange(slot_count)[None, :] < tile_count[:, None]
    kept = jnp.where(live_mask[:, :, None, None], adj_tiles, jnp.zeros((), jnp.bfloat16))
    picked = extended[tile_cols]
    fine_out = jnp.einsum("rkij,rkjf->rif", kept, picked, preferred_element_type=jnp.float32)
    fine_out = fine_out.reshape(vertex_rows, feat_width)
    total_sums, total_counts = lax.psum((coarse_sums, counts), ("dom", "grp"))
    coarse_all = finish(total_sums, total_counts, w_coarse)
    own_count = coarse_adj.shape[0]
    own_start = (lax.axis_index("dom") * lax.axis_size("grp") + lax.axis_index("grp")) * own_count
    self_rows = lax.dynamic_slice_in_dim(coarse_all, own_start, own_count, 0)
    coarse_mixed = (
        self_rows.astype(jnp.float32)
        + jnp.dot(coarse_adj, coarse_all, preferred_element_type=jnp.float32)
    ).astype(jnp.bfloat16)
    coarse_every = lax.all_gather(coarse_mixed, ("dom", "grp"), axis=0, tiled=True)
    return jax.nn.relu(fine_out + coarse_every[assign].astype(jnp.float32)).astype(jnp.bfloat16)


def solution(mesh):
    return jax.shard_map(
        per_device,
        mesh=mesh,
        in_specs=(
            P(("dom", "grp"), None),
            P(),
            P(("dom", "grp"), None, None, None),
            P(("dom", "grp"), None),
            P(("dom", "grp")),
            P(("dom", "grp")),
            P(("dom", "grp")),
            P(("dom", "grp")),
            P(),
            P(("dom", "grp"), None),
        ),
        out_specs=P(("dom", "grp"), None),
        check_vma=False,
    )
```

profile of v0, /device:TPU:0, one launch (start us, length us, event | category | flops | bytes accessed | tf_op | source)
XLA Modules:
  0.0 263.3 jit_solution(4760606489332169957)
XLA Ops:
  6.5 0.0 copy-start
  6.5 0.0 copy-start.8
  6.5 0.0 copy-start.4
  6.5 0.0 all-reduce.2.cloned.1.call-start
  6.5 0.7 compare_select_fusion.2
  7.2 0.2 copy-done
  7.5 2.3 convolution_convert_fusion
  9.8 0.0 copy-start.2
  9.8 0.0 copy-start.5
  9.8 0.0 copy-start.6
  9.8 0.6 gather_fusion.1
  10.4 2.4 collective-permute-start.1
  12.8 0.0 copy-done.8
  12.8 0.6 gather_fusion
  13.4 0.1 collective-permute-start
  13.5 0.0 copy-done.4
  13.5 21.9 %scatter_custom_fusion = f32[1024,256]{1,0:T(8,128)} fusion(s32[4096]{0:T(1024)S(1)} %copy-done.4, bf16[4096,256]{1,0:T(8,128)(2,1)} %param.10, f32[]{:T(128)} %constant.14.clone.1), kind=kCustom, calls=%fused_computation.14 | custom fusion | flops 2097152 | bytes 3145732 | tf_op jit(solution)/shard_map/scatter-add | solution.py:56
  35.4 0.0 all-reduce.2.cloned.1.call-update
  35.4 0.0 copy-done.5
  35.4 0.1 copy.11
  35.5 0.1 reshape.59
  35.6 0.0 copy-done.6
  35.6 0.1 iota_compare_fusion
  35.7 28.8 %scatter_custom_fusion.1 = f32[1024]{0:T(1024)S(1)} fusion(s32[4096]{0:T(1024)S(1)} %copy-done.4, f32[4096]{0:T(1024)S(1)} %broadcast.23, f32[]{:T(128)} %constant.14.clone.1), kind=kCustom, calls=%fused_computation.32 | custom fusion | flops 4096 | bytes 4100 | tf_op jit(solution)/shard_map/scatter-add | solution.py:57
  64.5 40.2 %psum.15 = f32[1024]{0:T(1024)S(1)} all-reduce(f32[1024]{0:T(1024)S(1)} %scatter_custom_fusion.1), channel_id=1, replica_groups=mesh['dom'=4,'grp'=8] {'dom','grp'}, use_global_device_ids=true, to_apply=%region_3.4 | all-reduce | flops 1024 | bytes 8192 | tf_op jit(solution)/shard_map/psum | solution.py:63
  104.7 0.0 collective-permute-done.1
  104.7 0.0 collective-permute-done
  104.7 0.0 copy-done.2
  104.8 1.9 pad_maximum_fusion
  106.7 19.3 %gather_fusion.2 = bf16[640,128,256]{2,1,0:T(8,128)(2,1)} fusion(bf16[40,128,256]{2,1,0:T(8,128)(2,1)S(1)} %pad_maximum_fusion, s32[1024]{0:T(1024)S(1)} %pad_clamp_fusion), kind=kCustom, calls=%fused_computation.2 | custom fusion | bytes 83888640 | tf_op jit(solution)/shard_map/gather | solution.py:60
  126.0 0.0 copy-start.7
  126.0 0.0 copy-start.3
  126.0 23.5 %fusion = f32[32,128,256,1]{2,1,3,0:T(8,128)} fusion(bf16[32,20,128,256]{3,2,1,0:T(8,128)(2,1)} %bitcast.27, bf16[32,20,128,128]{3,2,1,0:T(8,128)(2,1)} %param.12, pred[32,20]{1,0:T(8,128)(4,1)S(1)} %iota_compare_fusion), kind=kOutput, calls=%fused_computation.6 | convolution fusion | flops 5379194880 | bytes 67109504 | tf_op jit(solution)/shard_map/rkij,rkjf->rif/dot_general | solution.py:61
  149.4 18.4 %all-reduce.2.cloned.1.call-done = f32[1024,256]{1,0:T(8,128)} async-done(((f32[1024,256]{1,0:T(8,128)}), f32[1024,256]{1,0:T(8,128)}) %all-reduce.2.cloned.1.call-update) | async-done | bytes 1048592 | tf_op jit(solution)/shard_map/psum | solution.py:63
  167.8 0.0 copy-done.7
  167.8 1.6 convolution_convert_fusion.1
  169.4 0.0 copy-done.3
  169.4 0.2 fusion.9
  169.6 68.2 %all_gather.3 = bf16[1024,256]{1,0:T(8,128)(2,1)S(1)} all-gather(bf16[32,256]{1,0:T(8,128)(2,1)S(1)} %fusion.9), channel_id=1, replica_groups=mesh['dom'=4,'grp'=8] {'dom','grp'}, dimensions={0}, use_global_device_ids=true | all-gather | bytes 540672 | tf_op jit(solution)/shard_map/all_gather | solution.py:72
  237.8 0.0 copy-start.1
  237.8 14.6 %gather_fusion.3 = bf16[4096,256]{1,0:T(8,128)(2,1)S(1)} fusion(bf16[1024,256]{1,0:T(8,128)(2,1)S(1)} %all_gather.3, s32[4096]{0:T(1024)S(1)} %fusion.11), kind=kCustom, calls=%fused_computation.3 | custom fusion | bytes 4210688 | tf_op jit(solution)/shard_map/gather | solution.py:73
  252.5 4.0 %fusion.5 = bf16[4096,256]{1,0:T(8,128)(2,1)} fusion(f32[32,128,256,1]{2,1,3,0:T(8,128)} %fusion, bf16[4096,256]{1,0:T(8,128)(2,1)S(1)} %gather_fusion.3), kind=kLoop, calls=%fused_computation.13 | loop fusion | flops 4194304 | bytes 8388608 | tf_op jit(solution)/shard_map/convert_element_type | solution.py:73
  256.5 0.0 copy-done.1
  (8 shorter events, 0.0 us)
Async XLA Ops:
  6.5 0.9 copy-start
  6.5 6.3 %copy-start.8 = (s32[4]{0:T(128)S(1)}, s32[4]{0:T(128)}, u32[]{:S(2)}) copy-start(s32[4]{0:T(128)} %param.16) | copy-start | bytes 52
  6.5 6.9 %copy-start.4 = (s32[4096]{0:T(1024)S(1)}, s32[4096]{0:T(1024)}, u32[]{:S(2)}) copy-start(s32[4096]{0:T(1024)} %param.17) | copy-start | bytes 49156
  6.5 161.3 %all-reduce.2.cloned.1.call-start = ((), (), s32[]{:S(2)}) async-start(), calls=%async_computation | async-start | bytes 2097152 | tf_op jit(solution)/shard_map/psum | solution.py:63
  9.8 95.0 %copy-start.2 = (bf16[4096,256]{1,0:T(8,128)(2,1)}, bf16[4096,256]{1,0:T(8,128)(2,1)S(1)}, u32[]{:S(2)}) copy-start(bf16[4096,256]{1,0:T(8,128)(2,1)S(1)} %convolution_convert_fusion) | copy-start | bytes 6291460
  9.8 25.6 %copy-start.5 = (s32[32,20]{0,1:T(8,128)S(1)}, s32[32,20]{0,1:T(8,128)}, u32[]{:S(2)}) copy-start(s32[32,20]{0,1:T(8,128)} %param.13) | copy-start | bytes 7684
  9.8 25.8 %copy-start.6 = (s32[32]{0:T(128)S(1)}, s32[32]{0:T(128)}, u32[]{:S(2)}) copy-start(s32[32]{0:T(128)} %param.14) | copy-start | bytes 388
  10.4 94.4 %collective-permute-start.1 = (bf16[512,256]{1,0:T(8,128)(2,1)S(1)}, bf16[512,256]{1,0:T(8,128)(2,1)S(1)}, u32[]{:S(2)}, u32[]{:S(2)}) collective-permute-start(bf16[512,256]{1,0:T(8,128)(2,1)S(1)} %bitcast.33), channel_id=1, source_target_pairs={{8,0},{16,8},{24,16},{0,24},{9,1},{17,9},{25,17},{1,25},{10,2},{18... | collective-permute-start | bytes 786440 | tf_op jit(solution)/shard_map/ppermute | solution.py:17
  13.4 91.3 %collective-permute-start = (bf16[512,256]{1,0:T(8,128)(2,1)S(1)}, bf16[512,256]{1,0:T(8,128)(2,1)S(1)}, u32[]{:S(2)}, u32[]{:S(2)}) collective-permute-start(bf16[512,256]{1,0:T(8,128)(2,1)S(1)} %bitcast.34), channel_id=1, source_target_pairs={{0,8},{8,16},{16,24},{24,0},{1,9},{9,17},{17,25},{25,1},{2,10},{10... | collective-permute-start | bytes 786440 | tf_op jit(solution)/shard_map/ppermute | solution.py:16
  126.0 41.9 %copy-start.7 = (bf16[256,256]{1,0:T(8,128)(2,1)S(1)}, bf16[256,256]{1,0:T(8,128)(2,1)}, u32[]{:S(2)}) copy-start(bf16[256,256]{1,0:T(8,128)(2,1)} %param.18) | copy-start | bytes 393220
  126.0 43.5 %copy-start.3 = (bf16[32,1024]{1,0:T(8,128)(2,1)S(1)}, bf16[32,1024]{1,0:T(8,128)(2,1)}, u32[]{:S(2)}) copy-start(bf16[32,1024]{1,0:T(8,128)(2,1)} %param.19) | copy-start | bytes 196612
  237.8 18.7 %copy-start.1 = (bf16[256,256]{1,0:T(8,128)(2,1)S(1)}, bf16[256,256]{1,0:T(8,128)(2,1)}, u32[]{:S(2)}) copy-start(bf16[256,256]{1,0:T(8,128)(2,1)} %param.11) | copy-start | bytes 393220
Sparse Core Ops, SparseCore 0:
  35.5 132.2 all-reduce.1
where the time goes:
time: 264 us; the launch traced here: 263 us
  blocking collectives  108 us (41%)
  other arithmetic  57.5 us (22%)
  local copies, waits for them, and re-layouts  35.4 us (13%)
  matrix products  27.6 us (10%)
  waiting for transfers between devices  18.4 us (7%)
  between operations  13.6 us (5%)
    all_gather x1, blocking collectives, per_device(): lax.all_gather(coarse_mixed, ('dom', 'grp'), axis=0, tiled=True)  68.2 us
    psum x1, blocking collectives, per_device(): total_sums, total_counts = lax.psum((coarse_sums, counts), ('dom', 'grp'))  40.2 us
    scatter-add x1, other arithmetic, per_device(): jax.ops.segment_sum(jnp.ones((vertex_rows,), jnp.float32), assign, num_se...  28.8 us
    dot_general x1, matrix products, per_device(): jnp.einsum('rkij,rkjf->rif', kept, picked, preferred_element_type=jnp.flo...  23.5 us
    scatter-add x1, other arithmetic, per_device(): jax.ops.segment_sum(features.astype(jnp.float32), assign, num_segments=NC)  21.9 us
    gather x1, local copies, waits for them, and re-layouts, per_device(): picked = extended[tile_cols]  19.3 us
    psum x1, waiting for transfers between devices, per_device(): total_sums, total_counts = lax.psum((coarse_sums, counts), ('dom', 'grp'))  18.4 us
    gather x1, local copies, waits for them, and re-layouts, per_device(): coarse_every[assign].astype(jnp.float32)  14.6 us
  transfers between devices with their start and end apart: 3, of which 1 were waited for; matrix products, arithmetic and copies ran while one was open for 37% of the time, Pallas kernels for 0%

commit v1 on v0

--- a/solution.py
+++ b/solution.py
@@ -60,7 +60,9 @@
     picked = extended[tile_cols]
     fine_out = jnp.einsum("rkij,rkjf->rif", kept, picked, preferred_element_type=jnp.float32)
     fine_out = fine_out.reshape(vertex_rows, feat_width)
-    total_sums, total_counts = lax.psum((coarse_sums, counts), ("dom", "grp"))
+    total_sums, total_counts = lax.psum(
+        lax.psum((coarse_sums, counts), axis_name="grp"), axis_name="dom"
+    )
     coarse_all = finish(total_sums, total_counts, w_coarse)
     own_count = coarse_adj.shape[0]
     own_start = (lax.axis_index("dom") * lax.axis_size("grp") + lax.axis_index("grp")) * own_count

time: 264 us -> 250 us (0.947)
  blocking collectives: 108 us -> 97.6 us
  waiting for transfers between devices: 18.4 us -> 15 us
    psum x1 -> x2, blocking collectives: 40.2 us -> 27.6 us  [the longest x1 21.8 us: per_device(): lax.psum((coarse_sums, counts), axis_name='grp')]
    psum x1 -> x2, waiting for transfers between devices: 18.4 us -> 14.9 us  [the longest x1 14.5 us: per_device(): lax.psum(lax.psum((coarse_sums, counts), axis_name='grp'), axis_name='dom')]
  transfers between devices with their start and end apart: 3 -> 4, of which waited for: 1 -> 2; matrix products, arithmetic and copies ran while one was open for 37% -> 39% of each run, Pallas kernels for 0% -> 0%
where the time goes in v1:
time: 250 us; the launch traced here: 249 us
  blocking collectives  97.6 us (39%)
  other arithmetic  57.4 us (23%)
  local copies, waits for them, and re-layouts  35.4 us (14%)
  matrix products  27.9 us (11%)
  waiting for transfers between devices  15 us (6%)
  between operations  13.6 us (5%)
  starting transfers between devices  2.55 us (1%)
    all_gather x1, blocking collectives, per_device(): lax.all_gather(coarse_mixed, ('dom', 'grp'), axis=0, tiled=True)  70 us
    scatter-add x1, other arithmetic, per_device(): jax.ops.segment_sum(jnp.ones((vertex_rows,), jnp.float32), assign, num_se...  28.8 us
    dot_general x1, matrix products, per_device(): jnp.einsum('rkij,rkjf->rif', kept, picked, preferred_element_type=jnp.flo...  23.8 us
    scatter-add x1, other arithmetic, per_device(): jax.ops.segment_sum(features.astype(jnp.float32), assign, num_segments=NC)  21.9 us
    psum x1, blocking collectives, per_device(): lax.psum((coarse_sums, counts), axis_name='grp')  21.8 us
    gather x1, local copies, waits for them, and re-layouts, per_device(): picked = extended[tile_cols]  19.3 us
    gather x1, local copies, waits for them, and re-layouts, per_device(): coarse_every[assign].astype(jnp.float32)  14.6 us
    psum x1, waiting for transfers between devices, per_device(): lax.psum(lax.psum((coarse_sums, counts), axis_name='grp'), axis_name='dom')  14.5 us
  transfers between devices with their start and end apart: 4, of which 2 were waited for; matrix products, arithmetic and copies ran while one was open for 39% of the time, Pallas kernels for 0%

profile of v1, /device:TPU:0, one launch (start us, length us, event | category | flops | bytes accessed | tf_op | source)
XLA Modules:
  0.0 249.4 jit_solution(9443433864067554659)
XLA Ops:
  6.5 0.0 copy-start
  6.5 0.0 copy-start.4
  6.5 0.0 all-reduce.3.cloned.1.call-start
  6.5 0.7 compare_select_fusion.2
  7.2 0.2 copy-done
  7.5 0.0 copy-start.8
  7.5 2.3 convolution_convert_fusion
  9.8 0.0 copy-start.2
  9.8 0.0 copy-start.5
  9.8 0.0 copy-start.6
  9.8 0.6 gather_fusion.1
  10.4 2.5 collective-permute-start.1
  12.8 0.0 copy-done.4
  12.8 21.9 %scatter_custom_fusion = f32[1024,256]{1,0:T(8,128)} fusion(s32[4096]{0:T(1024)S(1)} %copy-done.4, bf16[4096,256]{1,0:T(8,128)(2,1)} %param.10, f32[]{:T(128)} %constant.14.clone.1), kind=kCustom, calls=%fused_computation.14 | custom fusion | flops 2097152 | bytes 3145732 | tf_op jit(solution)/shard_map/scatter-add | solution.py:56
  34.7 0.0 all-reduce.3.cloned.1.call-update
  34.7 0.0 all-reduce.5.cloned.1.call-start
  34.8 0.0 copy-done.8
  34.8 0.6 gather_fusion
  35.4 0.1 collective-permute-start
  35.5 0.0 copy-done.5
  35.5 0.1 copy.11
  35.6 0.1 reshape.59
  35.7 0.0 copy-done.6
  35.7 0.1 iota_compare_fusion
  35.8 28.8 %scatter_custom_fusion.1 = f32[1024]{0:T(1024)S(1)} fusion(s32[4096]{0:T(1024)S(1)} %copy-done.4, f32[4096]{0:T(1024)S(1)} %broadcast.23, f32[]{:T(128)} %constant.14.clone.1), kind=kCustom, calls=%fused_computation.32 | custom fusion | flops 4096 | bytes 4100 | tf_op jit(solution)/shard_map/scatter-add | solution.py:57
  64.6 21.8 %psum.30 = f32[1024]{0:T(1024)S(1)} all-reduce(f32[1024]{0:T(1024)S(1)} %scatter_custom_fusion.1), channel_id=1, replica_groups=mesh['dom'=4,'grp'=8] {'grp'}, use_global_device_ids=true, to_apply=%region_4.5 | all-reduce | flops 1024 | bytes 8192 | tf_op jit(solution)/shard_map/psum | solution.py:64
  86.3 5.8 %psum.31 = f32[1024]{0:T(1024)S(1)} all-reduce(f32[1024]{0:T(1024)S(1)} %psum.30), channel_id=1, replica_groups=mesh['dom'=4,'grp'=8] {'dom'}, use_global_device_ids=true, to_apply=%region_5.6 | all-reduce | flops 1024 | bytes 8192 | tf_op jit(solution)/shard_map/psum | solution.py:63
  92.1 0.0 collective-permute-done.1
  92.2 0.0 collective-permute-done
  92.2 0.0 copy-done.2
  92.2 1.9 pad_maximum_fusion
  94.1 19.3 %gather_fusion.2 = bf16[640,128,256]{2,1,0:T(8,128)(2,1)} fusion(bf16[40,128,256]{2,1,0:T(8,128)(2,1)S(1)} %pad_maximum_fusion, s32[1024]{0:T(1024)S(1)} %pad_clamp_fusion), kind=kCustom, calls=%fused_computation.2 | custom fusion | bytes 83888640 | tf_op jit(solution)/shard_map/gather | solution.py:60
  113.4 0.5 all-reduce.3.cloned.1.call-done
  113.8 0.0 all-reduce.5.cloned.1.call-update
  113.8 0.0 copy-start.7
  113.8 0.0 copy-start.3
  113.9 23.8 %fusion = f32[32,128,256,1]{2,1,3,0:T(8,128)} fusion(bf16[32,20,128,256]{3,2,1,0:T(8,128)(2,1)} %bitcast.27, bf16[32,20,128,128]{3,2,1,0:T(8,128)(2,1)} %param.12, pred[32,20]{1,0:T(8,128)(4,1)S(1)} %iota_compare_fusion), kind=kOutput, calls=%fused_computation.6 | convolution fusion | flops 5379194880 | bytes 67109504 | tf_op jit(solution)/shard_map/rkij,rkjf->rif/dot_general | solution.py:61
  137.6 14.5 %all-reduce.5.cloned.1.call-done = f32[1024,256]{1,0:T(8,128)} async-done(((f32[1024,256]{1,0:T(8,128)}), f32[1024,256]{1,0:T(8,128)}) %all-reduce.5.cloned.1.call-update) | async-done | bytes 1048592 | tf_op jit(solution)/shard_map/psum | solution.py:63
  152.1 0.0 copy-done.7
  152.1 1.6 convolution_convert_fusion.1
  153.7 0.0 copy-done.3
  153.7 0.2 fusion.9
  153.9 70.0 %all_gather.3 = bf16[1024,256]{1,0:T(8,128)(2,1)S(1)} all-gather(bf16[32,256]{1,0:T(8,128)(2,1)S(1)} %fusion.9), channel_id=1, replica_groups=mesh['dom'=4,'grp'=8] {'dom','grp'}, dimensions={0}, use_global_device_ids=true | all-gather | bytes 540672 | tf_op jit(solution)/shard_map/all_gather | solution.py:74
  223.9 0.0 copy-start.1
  223.9 14.6 %gather_fusion.3 = bf16[4096,256]{1,0:T(8,128)(2,1)S(1)} fusion(bf16[1024,256]{1,0:T(8,128)(2,1)S(1)} %all_gather.3, s32[4096]{0:T(1024)S(1)} %fusion.11), kind=kCustom, calls=%fused_computation.3 | custom fusion | bytes 4210688 | tf_op jit(solution)/shard_map/gather | solution.py:75
  238.6 4.0 %fusion.5 = bf16[4096,256]{1,0:T(8,128)(2,1)} fusion(f32[32,128,256,1]{2,1,3,0:T(8,128)} %fusion, bf16[4096,256]{1,0:T(8,128)(2,1)S(1)} %gather_fusion.3), kind=kLoop, calls=%fused_computation.13 | loop fusion | flops 4194304 | bytes 8388608 | tf_op jit(solution)/shard_map/convert_element_type | solution.py:75
  242.6 0.0 copy-done.1
  (8 shorter events, 0.0 us)
Async XLA Ops:
  6.5 0.9 copy-start
  6.5 6.3 %copy-start.4 = (s32[4096]{0:T(1024)S(1)}, s32[4096]{0:T(1024)}, u32[]{:S(2)}) copy-start(s32[4096]{0:T(1024)} %param.17) | copy-start | bytes 49156
  6.5 107.3 %all-reduce.3.cloned.1.call-start = ((), (), s32[]{:S(2)}) async-start(), calls=%async_computation | async-start | bytes 2097152 | tf_op jit(solution)/shard_map/psum | solution.py:64
  7.5 27.3 %copy-start.8 = (s32[4]{0:T(128)S(1)}, s32[4]{0:T(128)}, u32[]{:S(2)}) copy-start(s32[4]{0:T(128)} %param.16) | copy-start | bytes 52
  9.8 82.4 %copy-start.2 = (bf16[4096,256]{1,0:T(8,128)(2,1)}, bf16[4096,256]{1,0:T(8,128)(2,1)S(1)}, u32[]{:S(2)}) copy-start(bf16[4096,256]{1,0:T(8,128)(2,1)S(1)} %convolution_convert_fusion) | copy-start | bytes 6291460
  9.8 25.7 %copy-start.5 = (s32[32,20]{0,1:T(8,128)S(1)}, s32[32,20]{0,1:T(8,128)}, u32[]{:S(2)}) copy-start(s32[32,20]{0,1:T(8,128)} %param.13) | copy-start | bytes 7684
  9.8 25.9 %copy-start.6 = (s32[32]{0:T(128)S(1)}, s32[32]{0:T(128)}, u32[]{:S(2)}) copy-start(s32[32]{0:T(128)} %param.14) | copy-start | bytes 388
  10.4 81.8 %collective-permute-start.1 = (bf16[512,256]{1,0:T(8,128)(2,1)S(1)}, bf16[512,256]{1,0:T(8,128)(2,1)S(1)}, u32[]{:S(2)}, u32[]{:S(2)}) collective-permute-start(bf16[512,256]{1,0:T(8,128)(2,1)S(1)} %bitcast.33), channel_id=1, source_target_pairs={{8,0},{16,8},{24,16},{0,24},{9,1},{17,9},{25,17},{1,25},{10,2},{18... | collective-permute-start | bytes 786440 | tf_op jit(solution)/shard_map/ppermute | solution.py:17
  34.7 117.4 %all-reduce.5.cloned.1.call-start = ((), (), s32[]{:S(2)}) async-start(), calls=%async_computation.1 | async-start | bytes 2097152 | tf_op jit(solution)/shard_map/psum | solution.py:63
  35.4 56.8 %collective-permute-start = (bf16[512,256]{1,0:T(8,128)(2,1)S(1)}, bf16[512,256]{1,0:T(8,128)(2,1)S(1)}, u32[]{:S(2)}, u32[]{:S(2)}) collective-permute-start(bf16[512,256]{1,0:T(8,128)(2,1)S(1)} %bitcast.34), channel_id=1, source_target_pairs={{0,8},{8,16},{16,24},{24,0},{1,9},{9,17},{17,25},{25,1},{2,10},{10... | collective-permute-start | bytes 786440 | tf_op jit(solution)/shard_map/ppermute | solution.py:16
  113.8 38.3 %copy-start.7 = (bf16[256,256]{1,0:T(8,128)(2,1)S(1)}, bf16[256,256]{1,0:T(8,128)(2,1)}, u32[]{:S(2)}) copy-start(bf16[256,256]{1,0:T(8,128)(2,1)} %param.18) | copy-start | bytes 393220
  113.8 39.8 %copy-start.3 = (bf16[32,1024]{1,0:T(8,128)(2,1)S(1)}, bf16[32,1024]{1,0:T(8,128)(2,1)}, u32[]{:S(2)}) copy-start(bf16[32,1024]{1,0:T(8,128)(2,1)} %param.19) | copy-start | bytes 196612
  223.9 18.7 %copy-start.1 = (bf16[256,256]{1,0:T(8,128)(2,1)S(1)}, bf16[256,256]{1,0:T(8,128)(2,1)}, u32[]{:S(2)}) copy-start(bf16[256,256]{1,0:T(8,128)(2,1)} %param.11) | copy-start | bytes 393220
Sparse Core Ops, SparseCore 0:
  34.9 78.8 all-reduce.2
  116.2 35.8 all-reduce.4
